TPU v7x, 32 devices: a whole 2x2x4 slice. The times are simulated.
32 devices in a mesh: dp: 4 (over y, x), expert: 8 (over z, core).
Axes of the slice: x: 2, y: 2, z: 4, core: 2. Of those that a mesh axis runs over, the one named last changes fastest.
Arguments:
- tokens: bfloat16 [4096, 4096], P(('dp', 'expert')), may hold values from -6 to 6
- routes: int32 [4096, 2], P(('dp', 'expert')), may hold values from 0 to 7, all different within a row; in each aligned block of 128 rows (0 to 127, 128 to 255, ...) at most 48 rows name the same one
- router_weight: bfloat16 [4096, 8], replicated, may hold values from -0.09375 to 0.09375
- shift: float32 [1, 4096], replicated, may hold values from -3 to 3
- scale: float32 [1, 4096], replicated, may hold values from -3 to 3
- gate_mod: float32 [1, 4096], replicated, may hold values from -4 to 4
- gate_weight: bfloat16 [8, 4096, 1024], P(None, ('dp', 'expert')), may hold values from -0.09375 to 0.09375
- up_weight: bfloat16 [8, 4096, 1024], P(None, ('dp', 'expert')), may hold values from -0.09375 to 0.09375
- down_weight: bfloat16 [8, 4096, 1024], P(None, ('dp', 'expert')), may hold values from -0.1875 to 0.1875
Outputs:
- update: bfloat16 [4096, 4096], P(('dp', 'expert'))
Inputs may be any that keep to these rules, and one draw needn't show every extreme that they name: `routes`: each row names two different experts; among the rows of one device no expert is named more than 48 times, a bound that some block reaches.
All inputs are finite; a program needn't handle non-finite values.
Results may differ from a plain program's by a relative error of at most 0.0072.
Values may be sent and summed in bfloat16 or wider, within the bound.
A program may use at most 128 MiB of HBM per device.

v0:
```python
import functools

import jax
import jax.numpy as jnp
from jax import lax
from jax.experimental import pallas as pl
from jax.experimental.pallas import tpu as pltpu
from jax.sharding import PartitionSpec as P

PIX = 4096


EPS = 1e-06

LAG, FAR = 1, 1
ISSUE = (1, 1)
FAR_TOKENS = 12
MULTIPLY = (13, 15)


def send_back(output):
    return lax.all_to_all(output, "expert", split_axis=0, concat_axis=0, tiled=True)


def shards_plain(
    tokens, routes, router_weight, shift, scale, gate_mod, gate_weight, up_weight, down_weight
):
    tok_dev = tokens.shape[0]
    width = tokens.shape[1]
    experts = router_weight.shape[1]
    n_owner = lax.axis_size("expert")
    local_count = experts // n_owner
    capacity = max(2, 3 * tok_dev // experts)
    first_row = (lax.axis_index("dp") * n_owner + lax.axis_index("expert")) * tok_dev
    image = first_row // PIX
    shift_row = lax.dynamic_slice_in_dim(shift, image, 1, 0)
    scale_row = lax.dynamic_slice_in_dim(scale, image, 1, 0)
    gate_row = lax.dynamic_slice_in_dim(gate_mod, image, 1, 0)
    values = tokens.astype(jnp.float32)
    meansq = jnp.mean(values * values, axis=-1, keepdims=True)
    normed = (values * lax.rsqrt(meansq + EPS) * (1.0 + scale_row) + shift_row).astype(jnp.bfloat16)
    logits = jnp.dot(normed, router_weight, preferred_element_type=jnp.float32)
    onehot = routes[:, :, None] == jnp.arange(experts, dtype=jnp.int32)[None, None, :]
    chosen = jnp.sum(jnp.where(onehot, logits[:, None, :], 0.0), axis=-1)
    score = jax.nn.sigmoid(chosen)
    flat = routes.reshape(-1)
    hot = (flat[:, None] == jnp.arange(experts, dtype=jnp.int32)[None, :]).astype(jnp.int32)
    rank = jnp.cumsum(hot, axis=0) - hot
    slot = jnp.sum(rank * hot, axis=-1)
    position = flat * capacity + slot
    source = (
        jnp.zeros((experts * capacity,), jnp.int32)
        .at[position]
        .set(jnp.arange(2 * tok_dev, dtype=jnp.int32) // 2)
    )
    filled = jnp.zeros((experts * capacity,), jnp.bool_).at[position].set(True)
    outgoing = jnp.where(filled[:, None], normed[source], jnp.zeros((), jnp.bfloat16)).reshape(
        experts, capacity, width
    )
    quarter_gate, quarter_up, quarter_down = (
        lax.all_to_all(gate_weight, "expert", split_axis=0, concat_axis=1, tiled=True),
        lax.all_to_all(up_weight, "expert", split_axis=0, concat_axis=1, tiled=True),
        lax.all_to_all(down_weight, "expert", split_axis=0, concat_axis=1, tiled=True),
    )
    w_gate, w_up, w_down = (
        lax.all_gather(quarter_gate, "dp", axis=1, tiled=True),
        lax.all_gather(quarter_up, "dp", axis=1, tiled=True),
        lax.all_gather(quarter_down, "dp", axis=1, tiled=True),
    )
    received = lax.all_to_all(outgoing, "expert", split_axis=0, concat_axis=0, tiled=True)
    slots = received.shape[1]
    grid = received.reshape(n_owner, local_count, slots, width)
    gate = jnp.einsum("nxcd,xdf->nxcf", grid, w_gate, preferred_element_type=jnp.float32)
    upper = jnp.einsum("nxcd,xdf->nxcf", grid, w_up, preferred_element_type=jnp.float32)
    hidden = (jax.nn.silu(gate) * upper).astype(jnp.bfloat16)
    output = jnp.einsum(
        "nxcf,xdf->nxcd", hidden, w_down, preferred_element_type=jnp.float32
    ).astype(jnp.bfloat16)
    output = output.reshape(n_owner * local_count, slots, width)
    incoming = send_back(output)
    picked = (
        incoming.reshape(experts * capacity, width)[position]
        .astype(jnp.float32)
        .reshape(tok_dev, 2, width)
    )
    branch = jnp.sum(score[:, :, None] * picked, axis=1)
    return (gate_row * branch).astype(jnp.bfloat16)


MESH = pl.DeviceIdType.MESH


def wait_bytes(ref, sem):
    pltpu.make_async_copy(ref, ref, sem).wait()


def kernel(
    n_dp, n_owner, tok_ref, router_ref, routes_ref, place_ref, shift_ref, scale_ref, gmod_ref,
    gate_ref, up_ref, down_ref, out_ref,
    weights, downs, normed, far_tok, meta, outgoing, rows, gate_acc, hidden, obuf, incoming, comb, dense, land,
    z_send, w_recv, xy_send, f_send, f_recv, t_send, t_recv, h_send, h_recv, o_send, o_recv, d_send, d_recv,
):
    dp, me = lax.axis_index("dp"), lax.axis_index("expert")
    x_dp = dp + 1 - 2 * (dp % 2)
    y_dp = (dp + 2) % n_dp
    d_dp = n_dp - 1 - dp
    n_half = n_owner // 2
    half, low = me // n_half, me % n_half
    other = 1 - half
    mirror = other * n_half + low
    tok_dev, width = tok_ref.shape
    capacity = outgoing.shape[2]
    depth, units = gate_ref.shape[1], gate_ref.shape[2]
    span = units
    last = 2

    def argument(a, expert):
        return (gate_ref, up_ref)[a].at[expert]

    barrier = pltpu.get_barrier_semaphore()
    for r in range(1, n_owner):
        pl.semaphore_signal(barrier, inc=1, device_id=(dp, (me + r) % n_owner), device_id_type=MESH)
    pl.semaphore_signal(barrier, inc=1, device_id=(x_dp, me), device_id_type=MESH)
    pl.semaphore_signal(barrier, inc=1, device_id=(y_dp, me), device_id_type=MESH)
    pl.semaphore_wait(barrier, n_owner + 1)

    def remote(src, dst, send_sem, recv_sem, to):
        return pltpu.make_async_remote_copy(
            src_ref=src, dst_ref=dst, send_sem=send_sem, recv_sem=recv_sem, device_id=to, device_id_type=MESH
        )

    def send_column(a):
        at = dp * n_owner + me
        pltpu.make_async_copy(argument(a, me), weights.at[a, at], w_recv.at[a, 0, 0]).start()
        for r in range(1, n_owner):
            to = ((half + r // n_half) % 2) * n_half + (low + r) % n_half
            remote(argument(a, to), weights.at[a, at], z_send.at[a], w_recv.at[a, r, 0], (dp, to)).start()

    def send_half():
        for b in range(2):
            for t in range(n_half):
                to = (low + t) % n_half
                src = down_ref.at[((half + b) % 2) * n_half + to]
                slot = b * n_half + low
                dst, arrive = downs.at[dp * n_owner + slot], w_recv.at[last, slot, 0]
                if t == 0:
                    pltpu.make_async_copy(src, dst, arrive).start()
                else:
                    remote(src, dst, z_send.at[last], arrive, (dp, half * n_half + to)).start()

    def piece(a, r, part):
        if a == last:
            return downs.at[part * n_owner + r]
        source = ((half + r // n_half) % 2) * n_half + (low + n_owner - r) % n_half
        return weights.at[a, part * n_owner + source]

    def spread(a, r, part, to, slot, kind):
        held = piece(a, r, part)
        remote(held, held, xy_send.at[a, kind], w_recv.at[a, r, slot], (to, me)).start()

    def arrived(a, r, part, slot):
        wait_bytes(piece(a, r, part), w_recv.at[a, r, slot])

    def relay(a, r):
        arrived(a, r, dp, 0)
        spread(a, r, dp, x_dp, 1, 0)
        spread(a, r, dp, y_dp, 2, 1)

    def corner(a, r):
        arrived(a, r, x_dp, 1)
        if r % 2 == 0:
            spread(a, r, x_dp, y_dp, 3, 2)
        arrived(a, r, y_dp, 2)
        if r % 2 == 1:
            spread(a, r, y_dp, x_dp, 3, 2)

    send_column(0)
    relay(0, 0)

    block = 16

    @pl.loop(0, tok_dev // block)
    def _(i):
        at = pl.ds(pl.multiple_of(i * block, block), block)
        values = tok_ref[at, :].astype(jnp.float32)
        meansq = jnp.mean(values * values, axis=-1, keepdims=True)
        fresh = values * lax.rsqrt(meansq + EPS) * (1.0 + scale_ref[...]) + shift_ref[...]
        normed[at, :] = fresh.astype(jnp.bfloat16)

    remote(normed, far_tok, f_send.at[0], f_recv.at[0], (dp, mirror)).start()
    logits = jnp.dot(normed[...], router_ref[...], preferred_element_type=jnp.float32)
    names = lax.broadcasted_iota(jnp.int32, logits.shape, 1)
    lanes = lax.broadcasted_iota(jnp.int32, meta.shape[1:], 1)
    facts = jnp.zeros(meta.shape[1:], jnp.float32)
    for k in range(2):
        chosen = jnp.sum(jnp.where(routes_ref[:, k : k + 1] == names, logits, 0.0), axis=-1, keepdims=True)
        facts = jnp.where(lanes == k, place_ref[:, k : k + 1].astype(jnp.float32), facts)
        facts = jnp.where(lanes == 2 + k, jax.nn.sigmoid(chosen), facts)
    meta[0] = facts
    remote(meta.at[0], meta.at[1], f_send.at[1], f_recv.at[1], (dp, mirror)).start()

    def dispatch(who):
        source = normed if who == 0 else far_tok
        from_half = half if who == 0 else other
        for t in range(n_half):
            to = (low + t) % n_half
            expert = half * n_half + to
            spots = (expert * capacity + lax.broadcasted_iota(jnp.int32, (tok_dev, capacity), 1)).astype(jnp.float32)
            first = jnp.where(meta[who, :, 0:1] == spots, 1.0, 0.0)
            second = jnp.where(meta[who, :, 1:2] == spots, 1.0, 0.0)
            hot = (first + second).astype(jnp.bfloat16)
            picked = lax.dot_general(
                hot, source[...], (((0,), (0,)), ((), ())), preferred_element_type=jnp.float32
            ).astype(jnp.bfloat16)
            if t == 0:
                rows[low, from_half] = picked
            else:
                outgoing[who, t - 1] = picked
                remote(
                    outgoing.at[who, t - 1], rows.at[low, from_half],
                    t_send.at[who], t_recv.at[who, t], (dp, expert),
                ).start()

    dispatch(0)

    def take_far():
        wait_bytes(far_tok, f_recv.at[0])
        wait_bytes(meta.at[1], f_recv.at[1])
        dispatch(1)
        for who in range(2):
            cells = lax.broadcasted_iota(jnp.int32, comb.shape[2:], 1).astype(jnp.float32)
            for k in range(2):
                comb[who, k] = jnp.where(meta[who, :, k : k + 1] == cells, 1.0, 0.0).astype(jnp.bfloat16)

    tile = 256

    def multiply(a):
        for r in range(n_owner):
            arrived(a, r, d_dp, 3)
        if a == 0:
            for who in range(2):
                from_half = half if who == 0 else other
                for t in range(1, n_half):
                    wait_bytes(rows.at[(low + n_half - t) % n_half, from_half], t_recv.at[who, t])

        @pl.loop(0, span // tile)
        def _(i):
            at = pl.ds(pl.multiple_of(i * tile, tile), tile)
            part = weights[a, :, :, at].reshape(width, tile)
            grid = rows[...].reshape(n_owner * capacity, width)
            result = jnp.dot(grid, part, preferred_element_type=jnp.float32)
            if a % 2 == 0:
                gate_acc[:, at] = result
            else:
                hidden[0, a // 2, :, at] = (jax.nn.silu(gate_acc[:, at]) * result).astype(jnp.bfloat16)

        if a % 2 == 1:
            remote(hidden.at[0, a // 2], hidden.at[1, a // 2], h_send.at[a // 2], h_recv.at[a // 2], (dp, mirror)).start()

    def finish(r):
        b, s = divmod(r, n_half)
        if r == n_half:
            for side in range(1):
                wait_bytes(hidden.at[1, side], h_recv.at[side])
        arrived(last, r, d_dp, 3)
        expert = ((half + b) % 2) * n_half + low
        for q in range(n_dp):
            total = jnp.zeros((n_owner * capacity, depth), jnp.float32)
            for side in range(1):
                total += lax.dot_general(
                    hidden[b, side], downs[q * n_owner + r, :, side * span : (side + 1) * span],
                    (((1,), (1,)), ((), ())), preferred_element_type=jnp.float32,
                )
            result = total.astype(jnp.bfloat16).reshape(n_half, 2, capacity, depth)
            obuf[r, :, :, :, q * depth : (q + 1) * depth] = result
        incoming[s, expert] = obuf[r, low]
        for t in range(1, n_half):
            to = (low + t) % n_half
            remote(
                obuf.at[r, to], incoming.at[s, expert],
                o_send.at[r], o_recv.at[s, b, t], (dp, half * n_half + to),
            ).start()

    def columns(q, part, s):
        return pl.ds(pl.multiple_of(((q * 2 + part) * n_half + s) * depth, depth), depth)

    def combine(s):
        for b in range(2):
            for t in range(1, n_half):
                sender = ((half + b) % 2) * n_half + (low + n_half - t) % n_half
                wait_bytes(incoming.at[s, sender], o_recv.at[s, b, t])
        for who in (1, 0):
            block_in = incoming[s, :, half if who == 0 else other].reshape(n_owner * capacity, n_dp * depth)
            first = jnp.dot(comb[who, 0], block_in, preferred_element_type=jnp.float32)
            second = jnp.dot(comb[who, 1], block_in, preferred_element_type=jnp.float32)
            branch = meta[who, :, 2:3] * first + meta[who, :, 3:4] * second
            for q in range(n_dp):
                at = columns(q, half, s)
                value = (gmod_ref[:, at] * branch[:, q * depth : (q + 1) * depth]).astype(jnp.bfloat16)
                if who == 0:
                    out_ref[:, at] = value
                else:
                    dense[s, :, q * depth : (q + 1) * depth] = value
            if who == 1:
                remote(dense.at[s], land.at[s], d_send.at[0], d_recv.at[s], (dp, mirror)).start()

    lag, far = LAG, FAR
    steps = [(a, r) for a in range(last + 1) for r in range(n_owner)]
    for k in range(1, len(steps) + lag + far):
        for a in range(1, last + 1):
            if k == ISSUE[a - 1]:
                send_half() if a == last else send_column(a)
        if k == FAR_TOKENS:
            take_far()
        if k < len(steps):
            relay(*steps[k])
        if lag <= k < len(steps) + lag:
            corner(*steps[k - lag])
        if k >= lag + far:
            a, r = steps[k - lag - far]
            for half_step in range(last):
                if (a * n_owner + r) == MULTIPLY[half_step]:
                    multiply(half_step)
            if a == last:
                finish(r)
                if r > n_half:
                    combine(r - n_half - 1)
    combine(n_half - 1)
    for s in range(n_half):
        wait_bytes(land.at[s], d_recv.at[s])
        for q in range(n_dp):
            out_ref[:, columns(q, other, s)] = land[s, :, q * depth : (q + 1) * depth]

    for a in range(last + 1):
        held = downs if a == last else weights.at[a]
        wait_bytes(held.at[pl.ds(0, n_owner - 2 if a == last else n_owner - 1)], z_send.at[a])
        for kind in range(3):
            wait_bytes(held.at[pl.ds(0, n_owner)], xy_send.at[a, kind])
    wait_bytes(normed, f_send.at[0])
    wait_bytes(meta.at[0], f_send.at[1])
    for who in range(2):
        wait_bytes(outgoing.at[who], t_send.at[who])
    for side in range(1):
        wait_bytes(hidden.at[0, side], h_send.at[side])
    for r in range(n_owner):
        wait_bytes(obuf.at[r, pl.ds(0, n_half - 1)], o_send.at[r])
    wait_bytes(dense, d_send.at[0])


def shards(
    n_dp, n_owner, tokens, routes, router_weight, shift, scale, gate_mod, gate_weight, up_weight, down_weight
):
    tok_dev, width = tokens.shape
    experts, depth, units = gate_weight.shape
    capacity = max(2, 3 * tok_dev // experts)
    first_row = (lax.axis_index("dp") * n_owner + lax.axis_index("expert")) * tok_dev
    image = first_row // PIX if shift.shape[0] > 1 else 0
    shift_row = lax.dynamic_slice_in_dim(shift, image, 1, 0)
    scale_row = lax.dynamic_slice_in_dim(scale, image, 1, 0)
    gate_row = lax.dynamic_slice_in_dim(gate_mod, image, 1, 0)
    hot = routes[:, :, None] == jnp.arange(experts, dtype=jnp.int32)[None, None, :]
    named = jnp.sum(hot.astype(jnp.bfloat16), axis=1)
    order = jnp.arange(tok_dev)
    below = (order[:, None] > order[None, :]).astype(jnp.bfloat16)
    rank = jnp.dot(below, named, preferred_element_type=jnp.float32)
    slot = jnp.sum(jnp.where(hot, rank[:, None, :], 0.0), axis=-1).astype(jnp.int32)
    place = routes * capacity + slot
    vmem = pl.BlockSpec(memory_space=pltpu.VMEM)
    hbm = pl.BlockSpec(memory_space=pl.ANY)
    grid_rows = n_owner * capacity
    n_half = n_owner // 2
    return pl.pallas_call(
        functools.partial(kernel, n_dp, n_owner),
        out_shape=jax.ShapeDtypeStruct((tok_dev, width), jnp.bfloat16),
        in_specs=[vmem] * 7 + [hbm] * 3,
        out_specs=vmem,
        scratch_shapes=[
            pltpu.VMEM((2, n_dp * n_owner, depth, units), jnp.bfloat16),
            pltpu.VMEM((n_dp * n_owner, depth, units), jnp.bfloat16),
            pltpu.VMEM((tok_dev, width), jnp.bfloat16),
            pltpu.VMEM((tok_dev, width), jnp.bfloat16),
            pltpu.VMEM((2, tok_dev, 128), jnp.float32),
            pltpu.VMEM((2, n_half - 1, capacity, width), jnp.bfloat16),
            pltpu.VMEM((n_half, 2, capacity, width), jnp.bfloat16),
            pltpu.VMEM((grid_rows, units), jnp.float32),
            pltpu.VMEM((2, 1, grid_rows, units), jnp.bfloat16),
            pltpu.VMEM((n_owner, n_half, 2, capacity, n_dp * depth), jnp.bfloat16),
            pltpu.VMEM((n_half, n_owner, 2, capacity, n_dp * depth), jnp.bfloat16),
            pltpu.VMEM((2, 2, tok_dev, grid_rows), jnp.bfloat16),
            pltpu.VMEM((n_half, tok_dev, n_dp * depth), jnp.bfloat16),
            pltpu.VMEM((n_half, tok_dev, n_dp * depth), jnp.bfloat16),
            pltpu.SemaphoreType.DMA((3,)),
            pltpu.SemaphoreType.DMA((3, n_owner, 4)),
            pltpu.SemaphoreType.DMA((3, 3)),
            pltpu.SemaphoreType.DMA((2,)),
            pltpu.SemaphoreType.DMA((2,)),
            pltpu.SemaphoreType.DMA((2,)),
            pltpu.SemaphoreType.DMA((2, n_half)),
            pltpu.SemaphoreType.DMA((1,)),
            pltpu.SemaphoreType.DMA((1,)),
            pltpu.SemaphoreType.DMA((n_owner,)),
            pltpu.SemaphoreType.DMA((n_half, 2, n_half)),
            pltpu.SemaphoreType.DMA((1,)),
            pltpu.SemaphoreType.DMA((n_half,)),
        ],
        compiler_params=pltpu.CompilerParams(
            collective_id=0, has_side_effects=True, vmem_limit_bytes=64000 * 1024
        ),
    )(
        tokens, router_weight, routes, place, shift_row, scale_row, gate_row,
        gate_weight, up_weight, down_weight,
    )


def choose(mesh):
    n_dp, n_owner = mesh.shape["dp"], mesh.shape["expert"]

    def body(*args):
        tokens, weight = args[0], args[6]
        capacity = max(2, 3 * tokens.shape[0] // weight.shape[0])
        fits = n_dp == 4 and weight.shape[0] == n_owner and n_owner % 2 == 0
        fits = fits and capacity % 16 == 0 and weight.shape[1] % 128 == 0 and tokens.shape[0] % 16 == 0
        fits = fits and weight.shape[2] % 512 == 0 and PIX % (n_owner * tokens.shape[0]) == 0
        if fits:
            return shards(n_dp, n_owner, *args)
        return shards_plain(*args)

    return body


def solution(mesh):
    in_specs = (
        P(("dp", "expert"), None),
        P(("dp", "expert"), None),
        P(),
        P(),
        P(),
        P(),
        P(None, ("dp", "expert"), None),
        P(None, ("dp", "expert"), None),
        P(None, ("dp", "expert"), None),
    )
    out_specs = P(("dp", "expert"), None)
    return jax.shard_map(
        choose(mesh), mesh=mesh, in_specs=in_specs, out_specs=out_specs, check_vma=False)
```

profile of v0, /device:TPU:28, one launch (start us, length us, event | category | flops | bytes accessed | tf_op | source)
XLA Modules:
  0.0 265.5 jit_solution(14247966916743081509)
XLA Ops:
  0.0 0.7 fusion.2
  0.7 0.1 fusion
  0.8 0.7 select_reduce_fusion
  1.5 0.7 convert_add_fusion
  2.2 0.7 copy.23.place_ref
  2.9 1.4 copy.22.routes_ref
  4.3 2.2 copy.21.router_ref
  6.5 256.7 %shard_map.91 = bf16[128,4096]{1,0:T(8,128)(2,1)} custom-call(bf16[128,4096]{1,0:T(8,128)(2,1)} %tok_ref.1, bf16[4096,8]{1,0:T(8,128)(2,1)} %copy.21.router_ref, s32[128,2]{1,0:T(8,128)} %copy.22.routes_ref, s32[128,2]{1,0:T(8,128)} %copy.23.place_ref, f32[1,4096]{1,0:T(1,128)} %shift_ref.1, f32[1,4096]{1,0:T(1,128)} %scale_ref.1, f32[1,4096]{1,0:T(1,128)} %gmod_ref.1, ...), custom_call_target="tpu_custom_call" | custom-call | tf_op jit(solution)/shard_map/pallas_call | solution.py:372
  263.2 2.3 copy.25
where the time goes:
time: 269 us; the launch traced here: 266 us
  Pallas kernels  257 us (96%)
  local copies, waits for them, and re-layouts  6.57 us (2%)
    pallas_call x1, Pallas kernels, shards(): pl.pallas_call(functools.partial(kernel, n_dp, n_owner), out_shape=jax.Sh...  257 us
    unnamed x3, local copies, waits for them, and re-layouts  5.84 us

commit v1 on v0

v1 whole, which is shorter than its diff:
```python
import functools

import jax
import jax.numpy as jnp
from jax import lax
from jax.experimental import pallas as pl
from jax.experimental.pallas import tpu as pltpu
from jax.sharding import PartitionSpec as P

PIX = 4096


EPS = 1e-06

ROWS = 32
LAG_B, LAG_C, LAG_G = 3, 4, 5
LAG_R1, LAG_R2, LAG_R3 = 6, 7, 8
LAG_M, LAG_O1, LAG_O2, LAG_O3 = 11, 12, 13, 14
DOWN_AT = 2


def send_back(output):
    return lax.all_to_all(output, "expert", split_axis=0, concat_axis=0, tiled=True)


def shards_plain(
    tokens, routes, router_weight, shift, scale, gate_mod, gate_weight, up_weight, down_weight
):
    tok_dev = tokens.shape[0]
    width = tokens.shape[1]
    experts = router_weight.shape[1]
    n_owner = lax.axis_size("expert")
    local_count = experts // n_owner
    capacity = max(2, 3 * tok_dev // experts)
    first_row = (lax.axis_index("dp") * n_owner + lax.axis_index("expert")) * tok_dev
    image = first_row // PIX
    shift_row = lax.dynamic_slice_in_dim(shift, image, 1, 0)
    scale_row = lax.dynamic_slice_in_dim(scale, image, 1, 0)
    gate_row = lax.dynamic_slice_in_dim(gate_mod, image, 1, 0)
    values = tokens.astype(jnp.float32)
    meansq = jnp.mean(values * values, axis=-1, keepdims=True)
    normed = (values * lax.rsqrt(meansq + EPS) * (1.0 + scale_row) + shift_row).astype(jnp.bfloat16)
    logits = jnp.dot(normed, router_weight, preferred_element_type=jnp.float32)
    onehot = routes[:, :, None] == jnp.arange(experts, dtype=jnp.int32)[None, None, :]
    chosen = jnp.sum(jnp.where(onehot, logits[:, None, :], 0.0), axis=-1)
    score = jax.nn.sigmoid(chosen)
    flat = routes.reshape(-1)
    hot = (flat[:, None] == jnp.arange(experts, dtype=jnp.int32)[None, :]).astype(jnp.int32)
    rank = jnp.cumsum(hot, axis=0) - hot
    slot = jnp.sum(rank * hot, axis=-1)
    position = flat * capacity + slot
    source = (
        jnp.zeros((experts * capacity,), jnp.int32)
        .at[position]
        .set(jnp.arange(2 * tok_dev, dtype=jnp.int32) // 2)
    )
    filled = jnp.zeros((experts * capacity,), jnp.bool_).at[position].set(True)
    outgoing = jnp.where(filled[:, None], normed[source], jnp.zeros((), jnp.bfloat16)).reshape(
        experts, capacity, width
    )
    quarter_gate, quarter_up, quarter_down = (
        lax.all_to_all(gate_weight, "expert", split_axis=0, concat_axis=1, tiled=True),
        lax.all_to_all(up_weight, "expert", split_axis=0, concat_axis=1, tiled=True),
        lax.all_to_all(down_weight, "expert", split_axis=0, concat_axis=1, tiled=True),
    )
    w_gate, w_up, w_down = (
        lax.all_gather(quarter_gate, "dp", axis=1, tiled=True),
        lax.all_gather(quarter_up, "dp", axis=1, tiled=True),
        lax.all_gather(quarter_down, "dp", axis=1, tiled=True),
    )
    received = lax.all_to_all(outgoing, "expert", split_axis=0, concat_axis=0, tiled=True)
    slots = received.shape[1]
    grid = received.reshape(n_owner, local_count, slots, width)
    gate = jnp.einsum("nxcd,xdf->nxcf", grid, w_gate, preferred_element_type=jnp.float32)
    upper = jnp.einsum("nxcd,xdf->nxcf", grid, w_up, preferred_element_type=jnp.float32)
    hidden = (jax.nn.silu(gate) * upper).astype(jnp.bfloat16)
    output = jnp.einsum(
        "nxcf,xdf->nxcd", hidden, w_down, preferred_element_type=jnp.float32
    ).astype(jnp.bfloat16)
    output = output.reshape(n_owner * local_count, slots, width)
    incoming = send_back(output)
    picked = (
        incoming.reshape(experts * capacity, width)[position]
        .astype(jnp.float32)
        .reshape(tok_dev, 2, width)
    )
    branch = jnp.sum(score[:, :, None] * picked, axis=1)
    return (gate_row * branch).astype(jnp.bfloat16)


MESH = pl.DeviceIdType.MESH
F32, BF16 = jnp.float32, jnp.bfloat16


def wait_bytes(ref, sem):
    pltpu.make_async_copy(ref, ref, sem).wait()


def kernel(
    tok_ref, router_ref, routes_ref, shift_ref, scale_ref, gmod_ref, gate_ref, up_ref, down_ref, out_ref,
    pieces, grid, weights, downs, meta, facts_col, part, from_outer, summed, from_mid, hidden, masked,
    sums, from_core, added, from_first, paired, from_second, final, land, gmod_z,
    sent, w_recv, m_recv, z_recv, x_recv, y_recv, d_recv, c_recv, o_recv, mid_recv, h_recv,
    core_recv, first_recv, second_recv, out_recv,
):
    dp, me = lax.axis_index("dp"), lax.axis_index("expert")
    n_z = pieces.shape[0]
    z, c = me // 2, me % 2
    x, y = dp % 2, dp // 2
    x_dp, y_dp, d_dp = dp + 1 - 2 * x, dp + 2 - 4 * y, 3 - dp
    mate = me + 1 - 2 * c
    spot, x_spot, y_spot, d_spot = dp * 2 + c, x_dp * 2 + c, y_dp * 2 + c, d_dp * 2 + c
    tok_dev, width = tok_ref.shape
    experts, depth, units = gate_ref.shape
    chunks, n_spot, rows, dset = grid.shape
    n_j = tok_dev // rows
    block = depth
    unit = units // n_spot
    n_dp = n_spot // 2

    def remote(src, dst, send_sem, recv_sem, to):
        return pltpu.make_async_remote_copy(
            src_ref=src, dst_ref=dst, send_sem=send_sem, recv_sem=recv_sem, device_id=to, device_id_type=MESH
        )

    barrier = pltpu.get_barrier_semaphore()
    for t in range(1, n_spot):
        to = (spot + t) % n_spot
        pl.semaphore_signal(barrier, inc=1, device_id=(to // 2, z * 2 + to % 2), device_id_type=MESH)
    for t in range(1, n_z):
        for k in range(2):
            pl.semaphore_signal(barrier, inc=1, device_id=(dp, ((z + t) % n_z) * 2 + k), device_id_type=MESH)
    pl.semaphore_wait(barrier, n_spot - 1 + 2 * (n_z - 1))

    def own_rows(ref, w):
        return ref.at[:, pl.ds(pl.multiple_of(w * block, block), block), :]

    def send_weight(a):
        ref = (gate_ref, up_ref)[a]
        mine = weights.at[:, pl.ds(pl.multiple_of(spot * block, block), block), a * unit : (a + 1) * unit]

        def source(s):
            return ref.at[:, :, pl.ds(pl.multiple_of(s * unit, unit), unit)]

        pltpu.make_async_copy(source(spot), mine, w_recv.at[a]).start()
        for s in (x_dp * 2 + c, y_dp * 2 + 1 - c, d_dp * 2 + c, y_dp * 2 + c, x_dp * 2 + 1 - c, d_dp * 2 + 1 - c, dp * 2 + 1 - c):
            remote(source(s), mine, sent.at[a], w_recv.at[a], (s // 2, z * 2 + s % 2)).start()

    def send_down(e):
        mine = downs.at[
            pl.ds(pl.multiple_of(spot * block, block), block), pl.ds(pl.multiple_of(e * unit, unit), unit)
        ]

        def source(s):
            return down_ref.at[e, :, pl.ds(pl.multiple_of(s * unit, unit), unit)]

        pltpu.make_async_copy(source(spot), mine, w_recv.at[2]).start()
        for s in (x_dp * 2 + c, y_dp * 2 + 1 - c, d_dp * 2 + c, y_dp * 2 + c, x_dp * 2 + 1 - c, d_dp * 2 + 1 - c, dp * 2 + 1 - c):
            remote(source(s), mine, sent.at[2], w_recv.at[2], (s // 2, z * 2 + s % 2)).start()

    send_weight(0)

    fine = 16
    wide = 2 * block

    def home(z_to, d):
        return (d * n_z + z_to) * wide

    @pl.loop(0, n_j)
    def _(j):
        for b in range(rows // fine):
            at = pl.ds(pl.multiple_of(j * rows + b * fine, fine), fine)
            values = tok_ref[at, :].astype(F32)
            meansq = jnp.mean(values * values, axis=-1, keepdims=True)
            fresh = (values * lax.rsqrt(meansq + EPS) * (1.0 + scale_ref[...]) + shift_ref[...]).astype(BF16)
            for t in range(n_z):
                for d in range(n_dp):
                    pieces[t, at, d * wide : (d + 1) * wide] = fresh[:, home(t, d) : home(t, d) + wide]
        span = pl.ds(pl.multiple_of(j * rows, rows), rows)
        grid[j * n_z + z, spot] = pieces[z, span, :]
        for t in range(1, n_z):
            to = (z + t) % n_z
            remote(
                pieces.at[to, span, :], grid.at[j * n_z + z, spot], sent.at[3], z_recv.at[j * n_z + z], (dp, to * 2 + c)
            ).start()

    logits = jnp.zeros((tok_dev, experts), F32)
    for t in range(n_z):
        for d in range(n_dp):
            logits += jnp.dot(
                pieces[t, :, d * wide : (d + 1) * wide], router_ref[home(t, d) : home(t, d) + wide, :],
                preferred_element_type=F32,
            )
    names = lax.broadcasted_iota(jnp.int32, logits.shape, 1)
    lanes = lax.broadcasted_iota(jnp.int32, (tok_dev, 128), 1)
    facts = jnp.zeros((tok_dev, 128), F32)
    for k in range(2):
        chosen = jnp.sum(jnp.where(routes_ref[:, k : k + 1] == names, logits, 0.0), axis=-1, keepdims=True)
        facts = jnp.where(lanes == k, routes_ref[:, k : k + 1].astype(F32), facts)
        facts = jnp.where(lanes == 2 + k, jax.nn.sigmoid(chosen), facts)
    meta[me, dp] = facts.T[0:8, :]
    for to in (x_dp, y_dp, d_dp):
        remote(meta.at[me, dp], meta.at[me, dp], sent.at[4], m_recv.at[0], (to, me)).start()
    send_weight(1)
    for d in range(n_dp):
        gmod_z[:, d * wide : (d + 1) * wide] = gmod_ref[
            :, pl.ds(pl.multiple_of((d * n_z + z) * wide, wide), wide)
        ]
    wait_bytes(meta.at[me, pl.ds(0, n_dp - 1)], m_recv.at[0])
    for t in range(1, 2 * n_z):
        remote(meta.at[me], meta.at[me], sent.at[5], m_recv.at[1], (dp, (me + t) % (2 * n_z))).start()
    wait_bytes(meta.at[pl.ds(0, 2 * n_z - 1)], m_recv.at[1])

    @pl.loop(0, 2 * n_z)
    def _(e):
        for d in range(n_dp):
            column = meta[e, d].T
            for j in range(n_j):
                at = pl.ds(pl.multiple_of((d * 2 + e % 2) * rows, rows), rows)
                facts_col[j * n_z + e // 2, at, :] = column[j * rows : (j + 1) * rows, :]

    def stage_a(i):
        held = grid.at[i, spot]

        @pl.when(i % n_z != z)
        def _():
            wait_bytes(held, z_recv.at[i])

        remote(held, held, sent.at[6], x_recv.at[i], (x_dp, me)).start()
        remote(held, held, sent.at[6], y_recv.at[i], (y_dp, me)).start()
        remote(held, held, sent.at[6], c_recv.at[i], (dp, mate)).start()

    def stage_b(i):
        par = (i // n_z + i) % 2
        wait_bytes(grid.at[i, x_spot], x_recv.at[i])
        wait_bytes(grid.at[i, y_spot], y_recv.at[i])
        relayed = grid.at[i, x_spot + par * (y_spot - x_spot)]
        remote(relayed, relayed, sent.at[7], d_recv.at[i], (y_dp + par * (x_dp - y_dp), me)).start()
        for s in (x_spot, y_spot):
            remote(grid.at[i, s], grid.at[i, s], sent.at[7], c_recv.at[i], (dp, mate)).start()

    def stage_c(i):
        held = grid.at[i, d_spot]
        wait_bytes(held, d_recv.at[i])
        remote(held, held, sent.at[8], c_recv.at[i], (dp, mate)).start()

    total = n_spot * rows
    mid_f = 2 - z
    out_f = 1 - z // 3

    def stage_g(i):
        @pl.when(i == 0)
        def _():
            for a in range(2):
                wait_bytes(weights.at[:, :, a * unit : (a + 1) * unit], w_recv.at[a])

        wait_bytes(grid.at[i, pl.ds(0, n_dp)], c_recv.at[i])
        block_in = grid[i].reshape(total, dset)
        first = facts_col[i, :, 0:1]
        second = facts_col[i, :, 1:2]
        picked = [jnp.zeros((total, 2 * unit), F32)] * 2
        for e in range(experts):
            result = jnp.dot(block_in, weights[e], preferred_element_type=F32)
            picked = [jnp.where(who == float(e), result, old) for who, old in zip((first, second), picked)]
        for k in range(2):
            part[i, k] = picked[k].astype(BF16)

        @pl.when(z % 3 == 0)
        def _():
            to = (dp, (1 + z // 3) * 2 + c)
            for k in (out_f, 1 - out_f):
                remote(part.at[i, k], from_outer.at[i, k], sent.at[9], o_recv.at[i, k], to).start()

    def stage_r1(i):
        @pl.when(z % 3 != 0)
        def _():
            wait_bytes(from_outer.at[i, mid_f], o_recv.at[i, mid_f])
            summed[i] = (from_outer[i, mid_f].astype(F32) + part[i, mid_f].astype(F32)).astype(BF16)
            remote(summed.at[i], from_mid.at[i], sent.at[9], mid_recv.at[i], (dp, (3 - z) * 2 + c)).start()

    def stage_r2(i):
        @pl.when(z % 3 != 0)
        def _():
            own = 1 - mid_f
            wait_bytes(from_outer.at[i, own], o_recv.at[i, own])
            wait_bytes(from_mid.at[i], mid_recv.at[i])
            value = from_outer[i, own].astype(F32) + part[i, own].astype(F32) + from_mid[i].astype(F32)
            score = jnp.where(own == 0, facts_col[i, :, 2:3], facts_col[i, :, 3:4])
            hidden[i, own] = (jax.nn.silu(value[:, :unit]) * value[:, unit:] * score).astype(BF16)
            held = hidden.at[i, own]
            remote(held, held, sent.at[10], h_recv.at[i, own], (dp, (3 - z) * 2 + c)).start()
            remote(held, held, sent.at[10], h_recv.at[i, own], (dp, (z - 1) * 6 + c)).start()

    def stage_r3(i):
        @pl.when(z % 3 != 0)
        def _():
            held = hidden.at[i, mid_f]
            wait_bytes(held, h_recv.at[i, mid_f])
            remote(held, held, sent.at[10], h_recv.at[i, mid_f], (dp, (z - 1) * 6 + c)).start()

    tile = 256

    def stage_m(i):
        @pl.when(i == 0)
        def _():
            wait_bytes(downs, w_recv.at[2])

        @pl.when(z % 3 == 0)
        def _():
            for k in range(2):
                wait_bytes(hidden.at[i, k], h_recv.at[i, k])

        first = facts_col[i, :, 0:1]
        second = facts_col[i, :, 1:2]
        h_first, h_second = hidden[i, 0].astype(F32), hidden[i, 1].astype(F32)
        for e in range(experts):
            value = jnp.where(first == float(e), h_first, jnp.where(second == float(e), h_second, 0.0))
            masked[:, e * unit : (e + 1) * unit] = value.astype(BF16)
        for n in range(dset // tile):
            at = slice(n * tile, (n + 1) * tile)
            result = lax.dot_general(
                masked[...], downs[at, :], (((1,), (1,)), ((), ())), preferred_element_type=F32
            ).astype(BF16).reshape(n_dp, 2, rows, tile)
            for k in range(2):
                sums[i, k, :, :, at] = result[:, k]
        remote(sums.at[i, 1 - c], from_core.at[i], sent.at[11], core_recv.at[i], (dp, mate)).start()

    def parity(i):
        return (i // n_z + i) % 2

    def stage_o1(i):
        wait_bytes(from_core.at[i], core_recv.at[i])
        value = (sums[i, c].astype(F32) + from_core[i].astype(F32)).astype(BF16)
        added[i] = value.reshape(2, 2, rows, dset)

        @pl.when(parity(i) == 0)
        def _():
            remote(added.at[i, :, 1 - x], from_first.at[i], sent.at[12], first_recv.at[i], (x_dp, me)).start()

        @pl.when(parity(i) == 1)
        def _():
            remote(added.at[i, 1 - y], from_first.at[i], sent.at[12], first_recv.at[i], (y_dp, me)).start()

    def stage_o2(i):
        par = parity(i)
        wait_bytes(from_first.at[i], first_recv.at[i])
        for t in range(2):
            own_y = t + par * (y - t)
            own_x = x + par * (t - x)
            paired[i, t] = (added[i, own_y, own_x].astype(F32) + from_first[i, t].astype(F32)).astype(BF16)
        other = 1 - y + par * (y - x)
        to = (y_dp + par * (x_dp - y_dp), me)
        remote(paired.at[i, other], from_second.at[i], sent.at[13], second_recv.at[i], to).start()

    def stage_o3(i):
        par = parity(i)
        wait_bytes(from_second.at[i], second_recv.at[i])
        own = y + par * (x - y)
        value = paired[i, own].astype(F32) + from_second[i].astype(F32)
        final[i] = (value * gmod_z[...]).astype(BF16)
        j, to = i // n_z, i % n_z

        @pl.when(to == z)
        def _():
            land[j * n_z + z] = final[i]

        @pl.when(to != z)
        def _():
            remote(final.at[i], land.at[j * n_z + z], sent.at[14], out_recv.at[j * n_z + z], (dp, to * 2 + c)).start()

    stages = (
        (0, stage_a), (LAG_B, stage_b), (LAG_C, stage_c), (LAG_G, stage_g), (LAG_R1, stage_r1), (LAG_R2, stage_r2),
        (LAG_R3, stage_r3), (LAG_M, stage_m), (LAG_O1, stage_o1), (LAG_O2, stage_o2), (LAG_O3, stage_o3),
    )

    @pl.loop(0, chunks + LAG_O3)
    def _(t):
        for lag, stage in stages:
            if lag == LAG_B:
                @pl.when(jnp.logical_and(t >= DOWN_AT, t < DOWN_AT + experts))
                def _():
                    send_down(t - DOWN_AT)

            @pl.when(jnp.logical_and(t >= lag, t < chunks + lag))
            def _(lag=lag, stage=stage):
                stage(t - lag)

    for j in range(n_j):
        for t in range(1, n_z):
            i = j * n_z + (z + t) % n_z
            wait_bytes(land.at[i], out_recv.at[i])
    for t in range(n_z):
        for j in range(n_j):
            for d in range(n_dp):
                out_ref[j * rows : (j + 1) * rows, home(t, d) : home(t, d) + wide] = land[
                    j * n_z + t, :, d * wide : (d + 1) * wide
                ]

    for a in range(2):
        wait_bytes(weights.at[:, 0 : (n_spot - 1) * block, 0:unit], sent.at[a])
    wait_bytes(downs.at[0 : (n_spot - 1) * block, :], sent.at[2])
    wait_bytes(pieces.at[0 : n_z - 1], sent.at[3])
    wait_bytes(meta.at[0, 0 : n_dp - 1], sent.at[4])
    wait_bytes(meta.at[0 : 2 * n_z - 1], sent.at[5])
    wait_bytes(grid.at[:, 0:3], sent.at[6])
    wait_bytes(grid.at[:, 0:3], sent.at[7])
    wait_bytes(grid.at[:, 0], sent.at[8])

    @pl.when(z % 3 == 0)
    def _():
        wait_bytes(part, sent.at[9])

    @pl.when(z % 3 != 0)
    def _():
        wait_bytes(summed, sent.at[9])
        wait_bytes(hidden, sent.at[10])
        wait_bytes(hidden.at[:, 0], sent.at[10])

    wait_bytes(from_core, sent.at[11])
    wait_bytes(from_first, sent.at[12])
    wait_bytes(from_second, sent.at[13])
    wait_bytes(final.at[0 : chunks - n_j], sent.at[14])


def shards(
    n_z, rows, tokens, routes, router_weight, shift, scale, gate_mod, gate_weight, up_weight, down_weight
):
    tok_dev, width = tokens.shape
    experts, depth, units = gate_weight.shape
    n_spot = width // (depth * n_z)
    n_dp = n_spot // 2
    dset = n_spot * depth
    unit = units // n_spot
    chunks = n_z * tok_dev // rows
    total = n_spot * rows
    vmem = pl.BlockSpec(memory_space=pltpu.VMEM)
    hbm = pl.BlockSpec(memory_space=pl.ANY)
    dma = pltpu.SemaphoreType.DMA
    return pl.pallas_call(
        kernel,
        out_shape=jax.ShapeDtypeStruct((tok_dev, width), BF16),
        in_specs=[vmem] * 6 + [hbm] * 3,
        out_specs=vmem,
        scratch_shapes=[
            pltpu.VMEM((n_z, tok_dev, dset), BF16),
            pltpu.VMEM((chunks, n_spot, rows, dset), BF16),
            pltpu.VMEM((experts, dset, 2 * unit), BF16),
            pltpu.VMEM((dset, experts * unit), BF16),
            pltpu.VMEM((2 * n_z, n_dp, 8, tok_dev), F32),
            pltpu.VMEM((chunks, total, 8), F32),
            pltpu.VMEM((chunks, 2, total, 2 * unit), BF16),
            pltpu.VMEM((chunks, 2, total, 2 * unit), BF16),
            pltpu.VMEM((chunks, total, 2 * unit), BF16),
            pltpu.VMEM((chunks, total, 2 * unit), BF16),
            pltpu.VMEM((chunks, 2, total, unit), BF16),
            pltpu.VMEM((total, experts * unit), BF16),
            pltpu.VMEM((chunks, 2, n_dp, rows, dset), BF16),
            pltpu.VMEM((chunks, n_dp, rows, dset), BF16),
            pltpu.VMEM((chunks, 2, 2, rows, dset), BF16),
            pltpu.VMEM((chunks, 2, rows, dset), BF16),
            pltpu.VMEM((chunks, 2, rows, dset), BF16),
            pltpu.VMEM((chunks, rows, dset), BF16),
            pltpu.VMEM((chunks, rows, dset), BF16),
            pltpu.VMEM((chunks, rows, dset), BF16),
            pltpu.VMEM((1, dset), F32),
            dma((15,)),
            dma((3,)),
            dma((2,)),
            dma((chunks,)),
            dma((chunks,)),
            dma((chunks,)),
            dma((chunks,)),
            dma((chunks,)),
            dma((chunks, 2)),
            dma((chunks,)),
            dma((chunks, 2)),
            dma((chunks,)),
            dma((chunks,)),
            dma((chunks,)),
            dma((chunks,)),
        ],
        compiler_params=pltpu.CompilerParams(
            collective_id=0, has_side_effects=True, vmem_limit_bytes=65000 * 1024
        ),
    )(tokens, router_weight, routes, shift, scale, gate_mod, gate_weight, up_weight, down_weight)


def choose(mesh):
    n_dp, n_owner = mesh.shape["dp"], mesh.shape["expert"]

    def body(*args):
        tokens, shift, weight = args[0], args[3], args[6]
        n_spot = 2 * n_dp
        fits = n_dp == 4 and n_owner == 8 and shift.shape[0] == 1
        fits = fits and tokens.shape[0] == 128 and tokens.shape[1] == n_dp * n_owner * weight.shape[1]
        fits = fits and weight.shape[1] % 128 == 0 and weight.shape[2] == 128 * n_spot and weight.shape[0] <= 8
        if fits:
            return shards(n_owner // 2, ROWS, *args)
        return shards_plain(*args)

    return body


def solution(mesh):
    in_specs = (
        P(("dp", "expert"), None),
        P(("dp", "expert"), None),
        P(),
        P(),
        P(),
        P(),
        P(None, ("dp", "expert"), None),
        P(None, ("dp", "expert"), None),
        P(None, ("dp", "expert"), None),
    )
    out_specs = P(("dp", "expert"), None)
    return jax.shard_map(
        choose(mesh), mesh=mesh, in_specs=in_specs, out_specs=out_specs, check_vma=False)
```

time: 269 us -> 212 us (0.79); the launches traced: 266 us -> 212 us
  Pallas kernels: 257 us -> 206 us
    pallas_call x1, Pallas kernels: 257 us -> 206 us  [shards(): pl.pallas_call(kernel, out_shape=jax.ShapeDtypeStruct((tok_dev, width), B...]
where the time goes in v1:
time: 212 us
  Pallas kernels  206 us (97%)
  local copies, waits for them, and re-layouts  5.84 us (3%)
    pallas_call x1, Pallas kernels, shards(): pl.pallas_call(kernel, out_shape=jax.ShapeDtypeStruct((tok_dev, width), B...  206 us
    unnamed x3, local copies, waits for them, and re-layouts  5.84 us

profile of v1, /device:TPU:28, one launch (start us, length us, event | category | flops | bytes accessed | tf_op | source)
XLA Modules:
  0.0 211.8 jit_solution(15006094630698850584)
XLA Ops:
  0.0 1.4 copy.11.routes_ref
  1.4 2.2 %copy.10.router_ref = bf16[4096,8]{1,0:T(8,128)(2,1)} copy(bf16[4096,8]{0,1:T(8,128)(2,1)} %param.11) | data formatting | bytes 131072 | tf_op args[2]
  3.6 206.0 %shard_map.91 = bf16[128,4096]{1,0:T(8,128)(2,1)} custom-call(bf16[128,4096]{1,0:T(8,128)(2,1)} %tok_ref.1, bf16[4096,8]{1,0:T(8,128)(2,1)} %copy.10.router_ref, s32[128,2]{1,0:T(8,128)} %copy.11.routes_ref, f32[1,4096]{1,0:T(1,128)} %shift_ref.1, f32[1,4096]{1,0:T(1,128)} %scale_ref.1, f32[1,4096]{1,0:T(1,128)} %gmod_ref.1, bf16[8,128,1024]{2,1,0:T(8,128)(2,1)} %gate_ref.1, ...), custom_call_target="tpu_custom_call" | custom-call | tf_op jit(solution)/shard_map/pallas_call | solution.py:439
  209.5 2.3 %copy.13 = bf16[128,4096]{1,0:T(8,128)(2,1)} copy(bf16[128,4096]{1,0:T(8,128)(2,1)} %shard_map.91) | data formatting | bytes 2097152

commit v2 on v1

--- a/solution.py
+++ b/solution.py
@@ -13,10 +13,16 @@
 EPS = 1e-06
 
 ROWS = 32
-LAG_B, LAG_C, LAG_G = 3, 4, 5
-LAG_R1, LAG_R2, LAG_R3 = 6, 7, 8
-LAG_M, LAG_O1, LAG_O2, LAG_O3 = 11, 12, 13, 14
-DOWN_AT = 2
+LEAD = 2
+LAG_B, LAG_C, LAG_G = 2, 4, 5
+LAG_R = 1, 2, 3, 4, 5
+LAG_M = 9
+LAG_O = 1, 2, 3
+DOWN_AT, DOWN_STEP = 5, 1
+MULTIPLY_AT, SLOW = 14, 6
+TAIL = 13
+ORDER = ("a", "b", "down", "c", "g", "ra", "rb", "rc", "rd", "re", "o3", "o2", "o1", "m")
+RING, HOLD = 4, 8
 
 
 def send_back(output):
@@ -98,9 +104,9 @@
 
 def kernel(
     tok_ref, router_ref, routes_ref, shift_ref, scale_ref, gmod_ref, gate_ref, up_ref, down_ref, out_ref,
-    pieces, grid, weights, downs, meta, facts_col, part, from_outer, summed, from_mid, hidden, masked,
-    sums, from_core, added, from_first, paired, from_second, final, land, gmod_z,
-    sent, w_recv, m_recv, z_recv, x_recv, y_recv, d_recv, c_recv, o_recv, mid_recv, h_recv,
+    pieces, grid, weights, downs, meta, facts_col, part, part_out, passing, hidden, masked,
+    sums, sums_out, from_core, added, added_out, from_first, paired, paired_out, from_second, final, land, gmod_z,
+    sent, w_recv, m_recv, z_recv, x_recv, y_recv, d_recv, c_recv, pass_recv, h_recv,
     core_recv, first_recv, second_recv, out_recv,
 ):
     dp, me = lax.axis_index("dp"), lax.axis_index("expert")
@@ -184,21 +190,247 @@
                 pieces.at[to, span, :], grid.at[j * n_z + z, spot], sent.at[3], z_recv.at[j * n_z + z], (dp, to * 2 + c)
             ).start()
 
-    logits = jnp.zeros((tok_dev, experts), F32)
+    logits = jnp.zeros((experts, tok_dev), F32)
     for t in range(n_z):
         for d in range(n_dp):
-            logits += jnp.dot(
-                pieces[t, :, d * wide : (d + 1) * wide], router_ref[home(t, d) : home(t, d) + wide, :],
-                preferred_element_type=F32,
+            logits += lax.dot_general(
+                router_ref[:, home(t, d) : home(t, d) + wide], pieces[t, :, d * wide : (d + 1) * wide],
+                (((1,), (1,)), ((), ())), preferred_element_type=F32,
             )
-    names = lax.broadcasted_iota(jnp.int32, logits.shape, 1)
-    lanes = lax.broadcasted_iota(jnp.int32, (tok_dev, 128), 1)
-    facts = jnp.zeros((tok_dev, 128), F32)
+    names = lax.broadcasted_iota(jnp.int32, logits.shape, 0)
+    facts = [routes_ref[k : k + 1, :].astype(F32) for k in range(2)]
     for k in range(2):
-        chosen = jnp.sum(jnp.where(routes_ref[:, k : k + 1] == names, logits, 0.0), axis=-1, keepdims=True)
-        facts = jnp.where(lanes == k, routes_ref[:, k : k + 1].astype(F32), facts)
-        facts = jnp.where(lanes == 2 + k, jax.nn.sigmoid(chosen), facts)
-    meta[me, dp] = facts.T[0:8, :]
+        chosen = jnp.sum(jnp.where(routes_ref[k : k + 1, :] == names, logits, 0.0), axis=0, keepdims=True)
+        facts.append(jax.nn.sigmoid(chosen))
+    lines = lax.broadcasted_iota(jnp.int32, (8, tok_dev), 0)
+    table = jnp.zeros((8, tok_dev), F32)
+    for k in range(4):
+        table = jnp.where(lines == k, facts[k], table)
+    meta[me, dp] = table
+    def stage_a(i):
+        held = grid.at[i, spot]
+
+        @pl.when(i % n_z != z)
+        def _():
+            wait_bytes(held, z_recv.at[i])
+
+        remote(held, held, sent.at[6], x_recv.at[i], (x_dp, me)).start()
+        remote(held, held, sent.at[6], y_recv.at[i], (y_dp, me)).start()
+
+        @pl.when(i < LEAD)
+        def _():
+            remote(held, held, sent.at[6], d_recv.at[i], (d_dp, me)).start()
+
+        remote(held, held, sent.at[6], c_recv.at[i], (dp, mate)).start()
+
+    def stage_b(i):
+        par = (i // n_z + i) % 2
+        wait_bytes(grid.at[i, x_spot], x_recv.at[i])
+        wait_bytes(grid.at[i, y_spot], y_recv.at[i])
+
+        @pl.when(i >= LEAD)
+        def _():
+            relayed = grid.at[i, x_spot + par * (y_spot - x_spot)]
+            remote(relayed, relayed, sent.at[7], d_recv.at[i], (y_dp + par * (x_dp - y_dp), me)).start()
+
+        for s in (x_spot, y_spot):
+            remote(grid.at[i, s], grid.at[i, s], sent.at[7], c_recv.at[i], (dp, mate)).start()
+
+    def stage_c(i):
+        held = grid.at[i, d_spot]
+        wait_bytes(held, d_recv.at[i])
+        remote(held, held, sent.at[8], c_recv.at[i], (dp, mate)).start()
+
+    total = n_spot * rows
+    mid_a, mid_b, end_k = 2 - z, z - 1, z // 3
+    end_to, mid_to = 1 + z // 3, 3 - z
+    outer = (z - 1) * 3
+
+    def at_end(body):
+        pl.when(z % 3 == 0)(body)
+
+    def at_mid(body):
+        pl.when(z % 3 != 0)(body)
+
+    halves = [slice(h * (total // 2), (h + 1) * (total // 2)) for h in range(2)]
+
+    def pass_on(i, k, h, to):
+        remote(
+            part_out.at[i, k, halves[h]], passing.at[i, k, halves[h]], sent.at[9], pass_recv.at[i, k, h],
+            (dp, to * 2 + c),
+        ).start()
+
+    def give(i, k, h, to):
+        held = hidden.at[i, k, halves[h]]
+        remote(held, held, sent.at[10], h_recv.at[i, k, h], (dp, to * 2 + c)).start()
+
+    def take(i, k, h):
+        wait_bytes(hidden.at[i, k, halves[h]], h_recv.at[i, k, h])
+
+    def stage_g(i):
+        @pl.when(i == 0)
+        def _():
+            for a in range(2):
+                wait_bytes(weights.at[:, :, a * unit : (a + 1) * unit], w_recv.at[a])
+
+        wait_bytes(grid.at[i, pl.ds(0, n_dp)], c_recv.at[i])
+        block_in = grid[i].reshape(total, dset)
+        first = facts_col[i, :, 0:1]
+        second = facts_col[i, :, 1:2]
+        picked = [jnp.zeros((total, 2 * unit), F32)] * 2
+        for e in range(experts):
+            result = jnp.dot(block_in, weights[e], preferred_element_type=F32)
+            picked = [jnp.where(who == float(e), result, old) for who, old in zip((first, second), picked)]
+        for k in range(2):
+            part[i % HOLD, k] = picked[k]
+
+        @at_end
+        def _():
+            part_out[i, 1 - end_k] = part[i % HOLD, 1 - end_k].astype(BF16)
+            for h in range(2):
+                pass_on(i, 1 - end_k, h, end_to)
+
+    def add_on(i, k, to):
+        for h in range(2):
+            at = halves[h]
+            wait_bytes(passing.at[i, k, at], pass_recv.at[i, k, h])
+            part_out[i, k, at] = (passing[i, k, at].astype(F32) + part[i % HOLD, k, at]).astype(BF16)
+            pass_on(i, k, h, to)
+
+    def stage_ra(i):
+        at_mid(lambda: add_on(i, mid_a, mid_to))
+
+    def stage_rb(i):
+        at_mid(lambda: add_on(i, mid_b, outer))
+
+    def stage_rc(i):
+        @at_end
+        def _():
+            for h in range(2):
+                at = halves[h]
+                wait_bytes(passing.at[i, end_k, at], pass_recv.at[i, end_k, h])
+                value = passing[i, end_k, at].astype(F32) + part[i % HOLD, end_k, at]
+                score = jnp.where(end_k == 0, facts_col[i, at, 2:3], facts_col[i, at, 3:4])
+                hidden[i, end_k, at] = (jax.nn.silu(value[:, :unit]) * value[:, unit:] * score).astype(BF16)
+                give(i, end_k, h, end_to)
+
+                @pl.when(i >= TAIL)
+                def _():
+                    give(i, end_k, h, 3 - end_to)
+                    give(i, end_k, h, 3 - z)
+
+    def relay_hidden(i, k, to):
+        for h in range(2):
+            take(i, k, h)
+            give(i, k, h, to)
+
+    def stage_rd(i):
+        at_mid(lambda: relay_hidden(i, mid_b, mid_to))
+
+    def stage_re(i):
+        at_mid(lambda: relay_hidden(i, mid_a, outer))
+
+    tile = 256
+
+    def stage_m(i):
+        @pl.when(i == 0)
+        def _():
+            wait_bytes(downs, w_recv.at[2])
+
+        @pl.when(z % 3 == 0)
+        def _():
+            for h in range(2):
+                take(i, 1 - end_k, h)
+
+        @pl.when(jnp.logical_and(z % 3 != 0, i >= TAIL))
+        def _():
+            for k in range(2):
+                for h in range(2):
+                    take(i, k, h)
+
+        first = facts_col[i, :, 0:1]
+        second = facts_col[i, :, 1:2]
+        h_first, h_second = hidden[i, 0].astype(F32), hidden[i, 1].astype(F32)
+        for e in range(experts):
+            value = jnp.where(first == float(e), h_first, jnp.where(second == float(e), h_second, 0.0))
+            masked[:, e * unit : (e + 1) * unit] = value.astype(BF16)
+        for n in range(dset // tile):
+            at = slice(n * tile, (n + 1) * tile)
+            result = lax.dot_general(
+                masked[...], downs[at, :], (((1,), (1,)), ((), ())), preferred_element_type=F32
+            ).reshape(n_dp, 2, rows, tile)
+            sums[i % RING, :, :, at] = jnp.where(c == 0, result[:, 0], result[:, 1])
+            sums_out[i, :, :, at] = jnp.where(c == 0, result[:, 1], result[:, 0]).astype(BF16)
+        remote(sums_out.at[i], from_core.at[i], sent.at[11], core_recv.at[i], (dp, mate)).start()
+
+    def parity(i):
+        return (i // n_z + i) % 2
+
+    def stage_o1(i):
+        par = parity(i)
+        wait_bytes(from_core.at[i], core_recv.at[i])
+        for t in range(2):
+            own = (t + par * (y - t)) * 2 + x + par * (t - x)
+            away = (t + par * (1 - y - t)) * 2 + 1 - x + par * (t - 1 + x)
+            added_out[i, t] = (sums[i % RING, away] + from_core[i, away].astype(F32)).astype(BF16)
+            added[i % RING, t] = sums[i % RING, own] + from_core[i, own].astype(F32)
+        keep = y + par * (x - y)
+        for s in (1 - keep, keep):
+            remote(
+                added_out.at[i, s], from_first.at[i, s], sent.at[12], first_recv.at[i, s],
+                (x_dp + par * (y_dp - x_dp), me),
+            ).start()
+
+    def stage_o2(i):
+        par = parity(i)
+        own = y + par * (x - y)
+        wait_bytes(from_first.at[i, 1 - own], first_recv.at[i, 1 - own])
+        paired_out[i] = (added[i % RING, 1 - own] + from_first[i, 1 - own].astype(F32)).astype(BF16)
+        remote(
+            paired_out.at[i], from_second.at[i], sent.at[13], second_recv.at[i], (y_dp + par * (x_dp - y_dp), me)
+        ).start()
+        wait_bytes(from_first.at[i, own], first_recv.at[i, own])
+        paired[i % RING] = added[i % RING, own] + from_first[i, own].astype(F32)
+
+    def stage_o3(i):
+        wait_bytes(from_second.at[i], second_recv.at[i])
+        value = paired[i % RING] + from_second[i].astype(F32)
+        final[i] = (value * gmod_z[...]).astype(BF16)
+        j, to = i // n_z, i % n_z
+
+        @pl.when(to == z)
+        def _():
+            land[j * n_z + z] = final[i]
+
+        @pl.when(to != z)
+        def _():
+            remote(final.at[i], land.at[j * n_z + z], sent.at[14], out_recv.at[j * n_z + z], (dp, to * 2 + c)).start()
+
+    def even(t, lag, stage, count=chunks):
+        @pl.when(jnp.logical_and(t >= lag, t < count + lag))
+        def _():
+            stage(t - lag)
+
+    def paced(t, shift, stage):
+        start, twice, late = MULTIPLY_AT + shift, MULTIPLY_AT + SLOW + shift, LAG_M + shift
+        single = twice + MULTIPLY_AT - LAG_M
+
+        @pl.when(jnp.logical_and(t >= start, t < twice))
+        def _():
+            stage(t - start)
+
+        @pl.when(jnp.logical_and(t >= twice, t < single))
+        def _():
+            @pl.loop(0, 2)
+            def _(s):
+                stage(SLOW + 2 * (t - twice) + s)
+
+        @pl.when(jnp.logical_and(t >= single, t < chunks + late))
+        def _():
+            stage(t - late)
+
+    for i in range(LEAD):
+        stage_a(i)
     for to in (x_dp, y_dp, d_dp):
         remote(meta.at[me, dp], meta.at[me, dp], sent.at[4], m_recv.at[0], (to, me)).start()
     send_weight(1)
@@ -219,171 +451,39 @@
                 at = pl.ds(pl.multiple_of((d * 2 + e % 2) * rows, rows), rows)
                 facts_col[j * n_z + e // 2, at, :] = column[j * rows : (j + 1) * rows, :]
 
-    def stage_a(i):
-        held = grid.at[i, spot]
-
-        @pl.when(i % n_z != z)
-        def _():
-            wait_bytes(held, z_recv.at[i])
-
-        remote(held, held, sent.at[6], x_recv.at[i], (x_dp, me)).start()
-        remote(held, held, sent.at[6], y_recv.at[i], (y_dp, me)).start()
-        remote(held, held, sent.at[6], c_recv.at[i], (dp, mate)).start()
-
-    def stage_b(i):
-        par = (i // n_z + i) % 2
-        wait_bytes(grid.at[i, x_spot], x_recv.at[i])
-        wait_bytes(grid.at[i, y_spot], y_recv.at[i])
-        relayed = grid.at[i, x_spot + par * (y_spot - x_spot)]
-        remote(relayed, relayed, sent.at[7], d_recv.at[i], (y_dp + par * (x_dp - y_dp), me)).start()
-        for s in (x_spot, y_spot):
-            remote(grid.at[i, s], grid.at[i, s], sent.at[7], c_recv.at[i], (dp, mate)).start()
-
-    def stage_c(i):
-        held = grid.at[i, d_spot]
-        wait_bytes(held, d_recv.at[i])
-        remote(held, held, sent.at[8], c_recv.at[i], (dp, mate)).start()
-
-    total = n_spot * rows
-    mid_f = 2 - z
-    out_f = 1 - z // 3
-
-    def stage_g(i):
-        @pl.when(i == 0)
-        def _():
-            for a in range(2):
-                wait_bytes(weights.at[:, :, a * unit : (a + 1) * unit], w_recv.at[a])
-
-        wait_bytes(grid.at[i, pl.ds(0, n_dp)], c_recv.at[i])
-        block_in = grid[i].reshape(total, dset)
-        first = facts_col[i, :, 0:1]
-        second = facts_col[i, :, 1:2]
-        picked = [jnp.zeros((total, 2 * unit), F32)] * 2
-        for e in range(experts):
-            result = jnp.dot(block_in, weights[e], preferred_element_type=F32)
-            picked = [jnp.where(who == float(e), result, old) for who, old in zip((first, second), picked)]
-        for k in range(2):
-            part[i, k] = picked[k].astype(BF16)
-
-        @pl.when(z % 3 == 0)
-        def _():
-            to = (dp, (1 + z // 3) * 2 + c)
-            for k in (out_f, 1 - out_f):
-                remote(part.at[i, k], from_outer.at[i, k], sent.at[9], o_recv.at[i, k], to).start()
-
-    def stage_r1(i):
-        @pl.when(z % 3 != 0)
-        def _():
-            wait_bytes(from_outer.at[i, mid_f], o_recv.at[i, mid_f])
-            summed[i] = (from_outer[i, mid_f].astype(F32) + part[i, mid_f].astype(F32)).astype(BF16)
-            remote(summed.at[i], from_mid.at[i], sent.at[9], mid_recv.at[i], (dp, (3 - z) * 2 + c)).start()
-
-    def stage_r2(i):
-        @pl.when(z % 3 != 0)
-        def _():
-            own = 1 - mid_f
-            wait_bytes(from_outer.at[i, own], o_recv.at[i, own])
-            wait_bytes(from_mid.at[i], mid_recv.at[i])
-            value = from_outer[i, own].astype(F32) + part[i, own].astype(F32) + from_mid[i].astype(F32)
-            score = jnp.where(own == 0, facts_col[i, :, 2:3], facts_col[i, :, 3:4])
-            hidden[i, own] = (jax.nn.silu(value[:, :unit]) * value[:, unit:] * score).astype(BF16)
-            held = hidden.at[i, own]
-            remote(held, held, sent.at[10], h_recv.at[i, own], (dp, (3 - z) * 2 + c)).start()
-            remote(held, held, sent.at[10], h_recv.at[i, own], (dp, (z - 1) * 6 + c)).start()
-
-    def stage_r3(i):
-        @pl.when(z % 3 != 0)
-        def _():
-            held = hidden.at[i, mid_f]
-            wait_bytes(held, h_recv.at[i, mid_f])
-            remote(held, held, sent.at[10], h_recv.at[i, mid_f], (dp, (z - 1) * 6 + c)).start()
-
-    tile = 256
-
-    def stage_m(i):
-        @pl.when(i == 0)
-        def _():
-            wait_bytes(downs, w_recv.at[2])
-
-        @pl.when(z % 3 == 0)
-        def _():
-            for k in range(2):
-                wait_bytes(hidden.at[i, k], h_recv.at[i, k])
-
-        first = facts_col[i, :, 0:1]
-        second = facts_col[i, :, 1:2]
-        h_first, h_second = hidden[i, 0].astype(F32), hidden[i, 1].astype(F32)
-        for e in range(experts):
-            value = jnp.where(first == float(e), h_first, jnp.where(second == float(e), h_second, 0.0))
-            masked[:, e * unit : (e + 1) * unit] = value.astype(BF16)
-        for n in range(dset // tile):
-            at = slice(n * tile, (n + 1) * tile)
-            result = lax.dot_general(
-                masked[...], downs[at, :], (((1,), (1,)), ((), ())), preferred_element_type=F32
-            ).astype(BF16).reshape(n_dp, 2, rows, tile)
-            for k in range(2):
-                sums[i, k, :, :, at] = result[:, k]
-        remote(sums.at[i, 1 - c], from_core.at[i], sent.at[11], core_recv.at[i], (dp, mate)).start()
-
-    def parity(i):
-        return (i // n_z + i) % 2
-
-    def stage_o1(i):
-        wait_bytes(from_core.at[i], core_recv.at[i])
-        value = (sums[i, c].astype(F32) + from_core[i].astype(F32)).astype(BF16)
-        added[i] = value.reshape(2, 2, rows, dset)
-
-        @pl.when(parity(i) == 0)
-        def _():
-            remote(added.at[i, :, 1 - x], from_first.at[i], sent.at[12], first_recv.at[i], (x_dp, me)).start()
-
-        @pl.when(parity(i) == 1)
-        def _():
-            remote(added.at[i, 1 - y], from_first.at[i], sent.at[12], first_recv.at[i], (y_dp, me)).start()
-
-    def stage_o2(i):
-        par = parity(i)
-        wait_bytes(from_first.at[i], first_recv.at[i])
-        for t in range(2):
-            own_y = t + par * (y - t)
-            own_x = x + par * (t - x)
-            paired[i, t] = (added[i, own_y, own_x].astype(F32) + from_first[i, t].astype(F32)).astype(BF16)
-        other = 1 - y + par * (y - x)
-        to = (y_dp + par * (x_dp - y_dp), me)
-        remote(paired.at[i, other], from_second.at[i], sent.at[13], second_recv.at[i], to).start()
-
-    def stage_o3(i):
-        par = parity(i)
-        wait_bytes(from_second.at[i], second_recv.at[i])
-        own = y + par * (x - y)
-        value = paired[i, own].astype(F32) + from_second[i].astype(F32)
-        final[i] = (value * gmod_z[...]).astype(BF16)
-        j, to = i // n_z, i % n_z
-
-        @pl.when(to == z)
-        def _():
-            land[j * n_z + z] = final[i]
-
-        @pl.when(to != z)
-        def _():
-            remote(final.at[i], land.at[j * n_z + z], sent.at[14], out_recv.at[j * n_z + z], (dp, to * 2 + c)).start()
-
-    stages = (
-        (0, stage_a), (LAG_B, stage_b), (LAG_C, stage_c), (LAG_G, stage_g), (LAG_R1, stage_r1), (LAG_R2, stage_r2),
-        (LAG_R3, stage_r3), (LAG_M, stage_m), (LAG_O1, stage_o1), (LAG_O2, stage_o2), (LAG_O3, stage_o3),
-    )
-
-    @pl.loop(0, chunks + LAG_O3)
+    def send_ahead(t):
+        @pl.when(jnp.logical_and(t >= LEAD, t < chunks))
+        def _():
+            stage_a(t)
+
+    def send_downs(t):
+        ahead = t - DOWN_AT
+
+        @pl.when(jnp.logical_and(ahead >= 0, jnp.logical_and(ahead < experts * DOWN_STEP, ahead % DOWN_STEP == 0)))
+        def _():
+            send_down(ahead // DOWN_STEP)
+
+    steps = {
+        "a": send_ahead,
+        "b": lambda t: even(t, LAG_B, stage_b),
+        "down": send_downs,
+        "c": lambda t: even(t, LAG_C, stage_c),
+        "g": lambda t: even(t, LAG_G, stage_g),
+        "ra": lambda t: even(t, LAG_G + LAG_R[0], stage_ra),
+        "rb": lambda t: even(t, LAG_G + LAG_R[1], stage_rb),
+        "rc": lambda t: even(t, LAG_G + LAG_R[2], stage_rc),
+        "rd": lambda t: even(t, LAG_G + LAG_R[3], stage_rd, TAIL),
+        "re": lambda t: even(t, LAG_G + LAG_R[4], stage_re, TAIL),
+        "m": lambda t: paced(t, 0, stage_m),
+        "o1": lambda t: paced(t, LAG_O[0], stage_o1),
+        "o2": lambda t: paced(t, LAG_O[1], stage_o2),
+        "o3": lambda t: paced(t, LAG_O[2], stage_o3),
+    }
+
+    @pl.loop(LAG_B, chunks + LAG_M + LAG_O[2])
     def _(t):
-        for lag, stage in stages:
-            if lag == LAG_B:
-                @pl.when(jnp.logical_and(t >= DOWN_AT, t < DOWN_AT + experts))
-                def _():
-                    send_down(t - DOWN_AT)
-
-            @pl.when(jnp.logical_and(t >= lag, t < chunks + lag))
-            def _(lag=lag, stage=stage):
-                stage(t - lag)
+        for name in ORDER:
+            steps[name](t)
 
     for j in range(n_j):
         for t in range(1, n_z):
@@ -403,18 +503,21 @@
     wait_bytes(meta.at[0, 0 : n_dp - 1], sent.at[4])
     wait_bytes(meta.at[0 : 2 * n_z - 1], sent.at[5])
     wait_bytes(grid.at[:, 0:3], sent.at[6])
-    wait_bytes(grid.at[:, 0:3], sent.at[7])
+    wait_bytes(grid.at[0:LEAD, 0], sent.at[6])
+    wait_bytes(grid.at[:, 0:2], sent.at[7])
+    wait_bytes(grid.at[LEAD:chunks, 0], sent.at[7])
     wait_bytes(grid.at[:, 0], sent.at[8])
 
-    @pl.when(z % 3 == 0)
+    @at_end
     def _():
-        wait_bytes(part, sent.at[9])
-
-    @pl.when(z % 3 != 0)
+        wait_bytes(part_out.at[:, 0], sent.at[9])
+        wait_bytes(hidden.at[:, 0], sent.at[10])
+        wait_bytes(hidden.at[TAIL:chunks], sent.at[10])
+
+    @at_mid
     def _():
-        wait_bytes(summed, sent.at[9])
-        wait_bytes(hidden, sent.at[10])
-        wait_bytes(hidden.at[:, 0], sent.at[10])
+        wait_bytes(part_out, sent.at[9])
+        wait_bytes(hidden.at[0:TAIL], sent.at[10])
 
     wait_bytes(from_core, sent.at[11])
     wait_bytes(from_first, sent.at[12])
@@ -448,17 +551,19 @@
             pltpu.VMEM((dset, experts * unit), BF16),
             pltpu.VMEM((2 * n_z, n_dp, 8, tok_dev), F32),
             pltpu.VMEM((chunks, total, 8), F32),
+            pltpu.VMEM((HOLD, 2, total, 2 * unit), F32),
             pltpu.VMEM((chunks, 2, total, 2 * unit), BF16),
             pltpu.VMEM((chunks, 2, total, 2 * unit), BF16),
-            pltpu.VMEM((chunks, total, 2 * unit), BF16),
-            pltpu.VMEM((chunks, total, 2 * unit), BF16),
             pltpu.VMEM((chunks, 2, total, unit), BF16),
             pltpu.VMEM((total, experts * unit), BF16),
-            pltpu.VMEM((chunks, 2, n_dp, rows, dset), BF16),
+            pltpu.VMEM((RING, n_dp, rows, dset), F32),
             pltpu.VMEM((chunks, n_dp, rows, dset), BF16),
-            pltpu.VMEM((chunks, 2, 2, rows, dset), BF16),
+            pltpu.VMEM((chunks, n_dp, rows, dset), BF16),
+            pltpu.VMEM((RING, 2, rows, dset), F32),
             pltpu.VMEM((chunks, 2, rows, dset), BF16),
             pltpu.VMEM((chunks, 2, rows, dset), BF16),
+            pltpu.VMEM((RING, rows, dset), F32),
+            pltpu.VMEM((chunks, rows, dset), BF16),
             pltpu.VMEM((chunks, rows, dset), BF16),
             pltpu.VMEM((chunks, rows, dset), BF16),
             pltpu.VMEM((chunks, rows, dset), BF16),
@@ -471,18 +576,17 @@
             dma((chunks,)),
             dma((chunks,)),
             dma((chunks,)),
+            dma((chunks, 2, 2)),
+            dma((chunks, 2, 2)),
+            dma((chunks,)),
             dma((chunks, 2)),
-            dma((chunks,)),
-            dma((chunks, 2)),
-            dma((chunks,)),
-            dma((chunks,)),
             dma((chunks,)),
             dma((chunks,)),
         ],
         compiler_params=pltpu.CompilerParams(
             collective_id=0, has_side_effects=True, vmem_limit_bytes=65000 * 1024
         ),
-    )(tokens, router_weight, routes, shift, scale, gate_mod, gate_weight, up_weight, down_weight)
+    )(tokens, router_weight.T, routes.T, shift, scale, gate_mod, gate_weight, up_weight, down_weight)
 
 
 def choose(mesh):

time: 212 us -> 186 us (0.88)
  Pallas kernels: 206 us -> 184 us
  local copies, waits for them, and re-layouts: 5.84 us -> 2.29 us
    pallas_call x1, Pallas kernels: 206 us -> 184 us  [shards(): pl.pallas_call(kernel, out_shape=jax.ShapeDtypeStruct((tok_dev, width), B...]
    unnamed x3 -> x1, local copies, waits for them, and re-layouts: 5.84 us -> 2.29 us
where the time goes in v2:
time: 186 us
  Pallas kernels  184 us (99%)
  local copies, waits for them, and re-layouts  2.29 us (1%)
    pallas_call x1, Pallas kernels, shards(): pl.pallas_call(kernel, out_shape=jax.ShapeDtypeStruct((tok_dev, width), B...  184 us

profile of v2, /device:TPU:28, one launch (start us, length us, event | category | flops | bytes accessed | tf_op | source)
XLA Modules:
  0.0 186.2 jit_solution(6554641855790006155)
XLA Ops:
  0.0 183.9 %shard_map.91 = bf16[128,4096]{1,0:T(8,128)(2,1)} custom-call(bf16[128,4096]{1,0:T(8,128)(2,1)} %tok_ref.1, bf16[8,4096]{1,0:T(8,128)(2,1)} %bitcast.2, s32[2,128]{1,0:T(2,128)} %bitcast.3, f32[1,4096]{1,0:T(1,128)} %shift_ref.1, f32[1,4096]{1,0:T(1,128)} %scale_ref.1, f32[1,4096]{1,0:T(1,128)} %gmod_ref.1, bf16[8,128,1024]{2,1,0:T(8,128)(2,1)} %gate_ref.1, ...), custom_call_target="tpu_custom_call" | custom-call | tf_op jit(solution)/shard_map/pallas_call | solution.py:542
  183.9 2.3 %copy.11 = bf16[128,4096]{1,0:T(8,128)(2,1)} copy(bf16[128,4096]{1,0:T(8,128)(2,1)} %shard_map.91) | data formatting | bytes 2097152

commit v3 on v2

--- a/solution.py
+++ b/solution.py
@@ -21,6 +21,7 @@
 DOWN_AT, DOWN_STEP = 5, 1
 MULTIPLY_AT, SLOW = 14, 6
 TAIL = 13
+TILE = 256
 ORDER = ("a", "b", "down", "c", "g", "ra", "rb", "rc", "rd", "re", "o3", "o2", "o1", "m")
 RING, HOLD = 4, 8
 
@@ -330,7 +331,7 @@
     def stage_re(i):
         at_mid(lambda: relay_hidden(i, mid_a, outer))
 
-    tile = 256
+    tile = TILE
 
     def stage_m(i):
         @pl.when(i == 0)
@@ -480,7 +481,7 @@
         "o3": lambda t: paced(t, LAG_O[2], stage_o3),
     }
 
-    @pl.loop(LAG_B, chunks + LAG_M + LAG_O[2])
+    @pl.loop(min(LEAD, LAG_B), chunks + LAG_M + LAG_O[2])
     def _(t):
         for name in ORDER:
             steps[name](t)
@@ -489,8 +490,7 @@
         for t in range(1, n_z):
             i = j * n_z + (z + t) % n_z
             wait_bytes(land.at[i], out_recv.at[i])
-    for t in range(n_z):
-        for j in range(n_j):
+        for t in range(n_z):
             for d in range(n_dp):
                 out_ref[j * rows : (j + 1) * rows, home(t, d) : home(t, d) + wide] = land[
                     j * n_z + t, :, d * wide : (d + 1) * wide

time: 186 us -> 186 us (level)
  no operation moved by 1% of the time
where the time goes in v3:
time: 186 us
  Pallas kernels  184 us (99%)
  local copies, waits for them, and re-layouts  2.29 us (1%)
    pallas_call x1, Pallas kernels, shards(): pl.pallas_call(kernel, out_shape=jax.ShapeDtypeStruct((tok_dev, width), B...  184 us

profile of v3, /device:TPU:28, one launch (start us, length us, event | category | flops | bytes accessed | tf_op | source)
XLA Modules:
  0.0 186.1 jit_solution(7814729781241860161)
XLA Ops:
  0.0 183.8 %shard_map.91 = bf16[128,4096]{1,0:T(8,128)(2,1)} custom-call(bf16[128,4096]{1,0:T(8,128)(2,1)} %tok_ref.1, bf16[8,4096]{1,0:T(8,128)(2,1)} %bitcast.2, s32[2,128]{1,0:T(2,128)} %bitcast.3, f32[1,4096]{1,0:T(1,128)} %shift_ref.1, f32[1,4096]{1,0:T(1,128)} %scale_ref.1, f32[1,4096]{1,0:T(1,128)} %gmod_ref.1, bf16[8,128,1024]{2,1,0:T(8,128)(2,1)} %gate_ref.1, ...), custom_call_target="tpu_custom_call" | custom-call | tf_op jit(solution)/shard_map/pallas_call | solution.py:542
  183.8 2.3 %copy.11 = bf16[128,4096]{1,0:T(8,128)(2,1)} copy(bf16[128,4096]{1,0:T(8,128)(2,1)} %shard_map.91) | data formatting | bytes 2097152
